TPU v7x, 32 devices: a whole 2x2x4 slice. The times are simulated.
32 devices in a mesh: groups: 2 (over x), dev: 4 (over y, core), tp: 4 (over z).
Axes of the slice: x: 2, y: 2, z: 4, core: 2. Of those that a mesh axis runs over, the one named last changes fastest.
Arguments:
- hidden_states: bfloat16 [5120, 5120], P(('groups', 'dev'), 'tp'), parts along dimension 0, may hold values from -6 to 6
- norm_gain: bfloat16 [5120], replicated, may hold values from 0.25 to 1.75
- w_query: bfloat16 [5120, 5120], P('dev', 'tp'), may hold values from -2 to 2
- w_key: bfloat16 [5120, 1024], P('dev', 'tp'), may hold values from -2 to 2
- w_value: bfloat16 [5120, 1024], P('dev', 'tp'), may hold values from -0.078125 to 0.078125
- prompt_blocks: int32 [16], P('groups'), parts along dimension 0, may hold values from 1 to 3, 20 in all
- owner_map: int32 [40], P(('groups', 'dev')), parts along dimension 0, may hold values from 0 to 3, as said below
- slot_table: int32 [8, 8], P(('groups', 'dev')), parts along dimension 0, may hold values from 0 to 7, each once within a row
Outputs:
- context: bfloat16 [5120, 5120], P(('groups', 'dev'), 'tp'), parts along dimension 0
- kv_cache: bfloat16 [64, 128, 2048], P(('groups', 'dev'), None, 'tp'), parts along dimension 0
There are 2 independent parts, one for each index of `groups`. A program takes and returns all parts, laid end to end along the dimension named above; an argument that names none is the same for every part. Nothing has to cross between parts.
Inputs may be any that keep to these rules, and one draw needn't show every extreme that they name: `prompt_blocks`: the entries sum to 20. `owner_map`: each device's 5 blocks name any owner at most 2 times, and no owner receives more than 8 blocks; in every draw some owner receives 2 blocks from every device. `slot_table`: each row is a permutation of 0 to 7.
All inputs are finite; a program needn't handle non-finite values.
Results may differ from a plain program's by a relative error of at most 0.0079.
Values may be sent and summed in bfloat16 or wider, within the bound.
A program may use at most 128 MiB of HBM per device.

v0:
```python
import functools
import math

import jax
import jax.numpy as jnp
from jax import lax
from jax.experimental import pallas as pl
from jax.experimental.pallas import tpu as pltpu
from jax.sharding import PartitionSpec as P

HD = 128
BLOCK = 128
EPSILON = 1e-06
THETA = 1000000.0
CORES = 2
VMEM_LIMIT = 64 * 1024 * 1024 - 128 * 1024
MESH = pl.DeviceIdType.MESH


def rope(x, cos2, sin2):
    return x * cos2 + pltpu.roll(x, HD // 2, 1) * sin2


def project_kernel(
    sizes,
    h_ref,
    gain_ref,
    wq_ref,
    wk_ref,
    wv_ref,
    cos_ref,
    sin_ref,
    own_ref,
    q_out,
    kv_out,
    own_out,
    hid,
    normed,
    wqf,
    wkf,
    wvf,
    kvf,
    ownf,
    local_sem,
    h_send,
    h_recv,
    sib_send,
    sib_recv,
    y_send,
    y_recv,
    x_send,
    x_recv,
    ys_send,
    ys_recv,
    xs_send,
    xs_recv,
    kv_send,
    kv_recv,
    o_send,
    o_recv,
):
    n_groups, n_dev, n_tp, q_chunks, pieces = sizes
    g = lax.axis_index("groups")
    d = lax.axis_index("dev")
    t = lax.axis_index("tp")
    ny = n_dev // CORES
    y = d // CORES
    core = d % CORES
    sib = y * CORES + (CORES - 1 - core)
    right, left = (t + 1) % n_tp, (t + n_tp - 1) % n_tp
    tok, feat = h_ref.shape
    sends = []

    def remote(src, dst, ssem, rsem, where):
        return pltpu.make_async_remote_copy(
            src_ref=src, dst_ref=dst, send_sem=ssem, recv_sem=rsem,
            device_id=where, device_id_type=MESH,
        )

    def send(src, dst, ssem, rsem, where):
        copy = remote(src, dst, ssem, rsem, where)
        copy.start()
        sends.append(copy)

    def landed(region, ssem, rsem, where):
        remote(region, region, ssem, rsem, where).wait_recv()

    barrier = pltpu.get_barrier_semaphore()
    count = 0
    for o in range(1, n_dev):
        pl.semaphore_signal(
            barrier, inc=1, device_id={"dev": (d + o) % n_dev}, device_id_type=MESH)
        count += 1
    for o in range(1, n_groups):
        pl.semaphore_signal(
            barrier, inc=1, device_id={"groups": (g + o) % n_groups}, device_id_type=MESH)
        count += 1
    for nb in (left, right):
        pl.semaphore_signal(barrier, inc=1, device_id={"tp": nb}, device_id_type=MESH)
        count += 1
    pl.semaphore_wait(barrier, count)

    own_w = (wk_ref, wv_ref, wq_ref)
    full_w = (wkf, wvf, wqf)
    chunks = [(0, 0, 0), (1, 0, 1)] + [(2, c, 2 + c) for c in range(q_chunks)]
    n_chunks = (1, 1, q_chunks)

    def own_part(a, c):
        rows = own_w[a].shape[0]
        size = rows // n_groups // n_chunks[a]
        first = pl.multiple_of(g * (rows // n_groups) + c * size, size)
        return own_w[a].at[pl.ds(first, size)]

    def full_part(a, c, dev, group):
        rows = own_w[a].shape[0]
        size = rows // n_groups // n_chunks[a]
        first = pl.multiple_of(dev * rows + group * (rows // n_groups) + c * size, size)
        return full_w[a].at[pl.ds(first, size)]

    def full_rows(a, dev):
        rows = own_w[a].shape[0]
        return full_w[a].at[pl.ds(pl.multiple_of(dev * rows, rows), rows)]

    prow = tok // pieces
    half = pieces // 2

    def hid_piece(block, p):
        first = pl.multiple_of(block * feat, 128)
        return hid.at[pl.ds(p * prow, prow), pl.ds(first, feat)]

    def own_piece(p):
        return h_ref.at[pl.ds(p * prow, prow)]

    def hops(direction, p):
        far = p < half if direction == 0 else p >= half
        return n_tp // 2 if far else n_tp // 2 - 1

    order = (
        list(range(pieces)),
        list(range(half, pieces)) + list(range(half)),
    )
    nbr = (right, left)

    def source(direction, s):
        return (t - s + n_tp) % n_tp if direction == 0 else (t + s) % n_tp

    for a, c, k in chunks[:2]:
        for oy in range(1, ny):
            peer = ((y + oy) % ny) * CORES + core
            send(own_part(a, c), full_part(a, c, d, g), y_send.at[oy - 1, k],
                 y_recv.at[oy - 1, k], {"dev": peer})
    for i in range(pieces):
        for direction in range(2):
            p = order[direction][i]
            if hops(direction, p) >= 1:
                send(own_piece(p), hid_piece(t, p), h_send.at[direction, 0, p],
                     h_recv.at[direction, 0, p], {"tp": nbr[direction]})
    for a, c, k in chunks[2:]:
        for oy in range(1, ny):
            peer = ((y + oy) % ny) * CORES + core
            send(own_part(a, c), full_part(a, c, d, g), y_send.at[oy - 1, k],
                 y_recv.at[oy - 1, k], {"dev": peer})
    for a in range(3):
        send(own_w[a], full_rows(a, d), sib_send.at[a], sib_recv.at[a], {"dev": sib})
    for o in range(1, n_dev):
        send(own_ref, ownf.at[d], o_send.at[o - 1], o_recv.at[o - 1], {"dev": (d + o) % n_dev})
    locals_ = []
    for a in range(3):
        locals_.append(pltpu.make_async_copy(own_w[a], full_rows(a, d), local_sem.at[a]))
    locals_.append(pltpu.make_async_copy(
        h_ref, hid.at[:, pl.ds(pl.multiple_of(t * feat, 128), feat)], local_sem.at[3]))
    locals_.append(pltpu.make_async_copy(own_ref, ownf.at[d], local_sem.at[4]))
    for copy in locals_:
        copy.start()

    def y_step(a, c, k):
        for oy in range(1, ny):
            dev = ((y - oy + ny) % ny) * CORES + core
            part = full_part(a, c, dev, g)
            landed(part, y_send.at[oy - 1, k], y_recv.at[oy - 1, k], {"dev": dev})
            for og in range(1, n_groups):
                send(part, part, x_send.at[oy - 1, og - 1, k], x_recv.at[oy - 1, og - 1, k],
                     {"groups": (g + og) % n_groups})
            send(part, part, ys_send.at[oy - 1, k], ys_recv.at[oy - 1, k], {"dev": sib})

    def x_step(a, c, k):
        for oy in range(1, ny):
            dev = ((y - oy + ny) % ny) * CORES + core
            for og in range(1, n_groups):
                group = (g - og + n_groups) % n_groups
                part = full_part(a, c, dev, group)
                landed(part, x_send.at[oy - 1, og - 1, k], x_recv.at[oy - 1, og - 1, k],
                       {"groups": group})
                send(part, part, xs_send.at[oy - 1, og - 1, k], xs_recv.at[oy - 1, og - 1, k],
                     {"dev": sib})

    def sib_done(a, c, k):
        for oy in range(1, ny):
            dev = ((y - oy + ny) % ny) * CORES + (CORES - 1 - core)
            part = full_part(a, c, dev, g)
            landed(part, ys_send.at[oy - 1, k], ys_recv.at[oy - 1, k], {"dev": sib})
            for og in range(1, n_groups):
                part = full_part(a, c, dev, (g - og + n_groups) % n_groups)
                landed(part, xs_send.at[oy - 1, og - 1, k], xs_recv.at[oy - 1, og - 1, k],
                       {"dev": sib})

    def h_step(s):
        for i in range(pieces):
            for direction in range(2):
                p = order[direction][i]
                if hops(direction, p) >= s + 1:
                    block = hid_piece(source(direction, s), p)
                    landed(block, h_send.at[direction, s - 1, p],
                           h_recv.at[direction, s - 1, p], {"tp": nbr[1 - direction]})
                    send(block, block, h_send.at[direction, s, p],
                         h_recv.at[direction, s, p], {"tp": nbr[direction]})

    y_step(*chunks[0])
    y_step(*chunks[1])
    for s in range(1, n_tp // 2):
        h_step(s)
    for i in range(2, len(chunks)):
        y_step(*chunks[i])
        x_step(*chunks[i - 2])
    for i in range(pieces):
        for direction in range(2):
            p = order[direction][i]
            s = hops(direction, p)
            if s >= 1:
                landed(hid_piece(source(direction, s), p), h_send.at[direction, s - 1, p],
                       h_recv.at[direction, s - 1, p], {"tp": nbr[1 - direction]})
    for copy in locals_:
        copy.wait()

    def norm_rows(i, _):
        rows = pl.ds(pl.multiple_of(i * 16, 16), 16)
        x = hid[rows, :].astype(jnp.float32)
        square = jnp.sum(x * x, axis=1, keepdims=True) * (1.0 / (feat * n_tp))
        normed[rows, :] = (x * lax.rsqrt(square + EPSILON) * gain_ref[...]).astype(jnp.bfloat16)
        return 0

    lax.fori_loop(0, tok // 16, norm_rows, 0)

    kv_width = wk_ref.shape[1]
    mine = pl.ds(pl.multiple_of(d * tok, tok), tok)
    for a in (0, 1):
        landed(full_rows(a, sib), sib_send.at[a], sib_recv.at[a], {"dev": sib})
        sib_done(*chunks[a])
        proj = jnp.dot(normed[...], full_w[a][...], preferred_element_type=jnp.float32)
        for head in range(kv_width // HD):
            part = proj[:, head * HD:(head + 1) * HD]
            if a == 0:
                part = rope(part, cos_ref[...], sin_ref[...])
            kvf[mine, (2 * head + a) * HD:(2 * head + a + 1) * HD] = part.astype(jnp.bfloat16)
    for i in range(len(chunks) - 2, len(chunks)):
        x_step(*chunks[i])
    send(kvf.at[mine], kvf.at[mine], kv_send.at[0, 0], kv_recv.at[0, 0], {"dev": sib})
    for oy in range(1, ny):
        peer = ((y + oy) % ny) * CORES + core
        send(kvf.at[mine], kvf.at[mine], kv_send.at[0, oy], kv_recv.at[0, oy], {"dev": peer})
    landed(full_rows(2, sib), sib_send.at[2], sib_recv.at[2], {"dev": sib})
    for i in range(2, len(chunks)):
        sib_done(*chunks[i])

    q_width = wq_ref.shape[1]
    tile = 256 if q_width % 256 == 0 else HD

    def q_tile(i, _):
        columns = pl.ds(pl.multiple_of(i * tile, tile), tile)
        proj = jnp.dot(normed[...], wqf[:, columns], preferred_element_type=jnp.float32)
        parts = [
            rope(proj[:, j * HD:(j + 1) * HD], cos_ref[...], sin_ref[...]).astype(jnp.bfloat16)
            for j in range(tile // HD)
        ]
        q_out[:, columns] = parts[0] if len(parts) == 1 else jnp.concatenate(parts, axis=1)
        return 0

    lax.fori_loop(0, q_width // tile, q_tile, 0)

    def kv_rows(dev):
        return kvf.at[pl.ds(pl.multiple_of(dev * tok, tok), tok)]

    for oy in range(1, ny):
        dev = ((y - oy + ny) % ny) * CORES + core
        part = kv_rows(dev)
        landed(part, kv_send.at[0, oy], kv_recv.at[0, oy], {"dev": dev})
        send(part, part, kv_send.at[1, oy], kv_recv.at[1, oy], {"dev": sib})
    landed(kv_rows(sib), kv_send.at[0, 0], kv_recv.at[0, 0], {"dev": sib})
    for oy in range(1, ny):
        dev = ((y - oy + ny) % ny) * CORES + (CORES - 1 - core)
        landed(kv_rows(dev), kv_send.at[1, oy], kv_recv.at[1, oy], {"dev": sib})
    for o in range(1, n_dev):
        dev = (d - o + n_dev) % n_dev
        landed(ownf.at[dev], o_send.at[o - 1], o_recv.at[o - 1], {"dev": dev})
    for copy in sends:
        copy.wait_send()
    kv_out[...] = kvf[...]
    own_out[...] = ownf[...]


def attend_kernel(
    blk_dev, group_size, prompt_ref, owner_ref, slot_ref, dev_ref, q_ref, kv_ref, ctx_ref,
    cache_ref
):
    tok, q_width = q_ref.shape
    heads = q_width // HD
    kv_heads = heads // group_size
    d = dev_ref[0]
    n_prompts = prompt_ref.shape[0]
    scale = 1.0 / math.sqrt(HD)

    cache_ref[...] = jnp.zeros_like(cache_ref)

    def place(b, rank):
        hit = owner_ref[b] == d
        @pl.when(hit)
        def _():
            cache_ref[slot_ref[rank]] = kv_ref[pl.ds(pl.multiple_of(b * BLOCK, BLOCK), BLOCK), :]
        return rank + hit.astype(jnp.int32)

    lax.fori_loop(0, owner_ref.shape[0], place, jnp.int32(0))

    stacked = group_size * BLOCK
    row = lax.broadcasted_iota(jnp.int32, (group_size, BLOCK, BLOCK), 1).reshape(stacked, BLOCK)
    col = lax.broadcasted_iota(jnp.int32, (group_size, BLOCK, BLOCK), 2).reshape(stacked, BLOCK)
    causal = col <= row

    def q_block(b, _):
        block = d * blk_dev + b
        first = jnp.int32(0)
        total = jnp.int32(0)
        for p in range(n_prompts):
            first = jnp.where(total <= block, total, first)
            total = total + prompt_ref[p]
        rows = pl.ds(pl.multiple_of(b * BLOCK, BLOCK), BLOCK)
        for kh in range(kv_heads):
            q = jnp.concatenate(
                [
                    q_ref[rows, (kh * group_size + j) * HD:(kh * group_size + j + 1) * HD]
                    for j in range(group_size)
                ],
                axis=0,
            )

            def scores_of(j):
                at = pl.ds(pl.multiple_of(j * BLOCK, BLOCK), BLOCK)
                keys = kv_ref[at, 2 * kh * HD:(2 * kh + 1) * HD]
                values = kv_ref[at, (2 * kh + 1) * HD:(2 * kh + 2) * HD]
                s = lax.dot_general(
                    q, keys, (((1,), (1,)), ((), ())), preferred_element_type=jnp.float32
                ) * scale
                return s, values

            s, values = scores_of(block)
            s = jnp.where(causal, s, -1e30)
            m = jnp.max(s, axis=1, keepdims=True)
            w = jnp.where(causal, jnp.exp(s - m), 0.0)
            l = jnp.sum(w, axis=1, keepdims=True)
            acc = jnp.dot(w.astype(jnp.bfloat16), values, preferred_element_type=jnp.float32)

            def step(j, carry):
                m, l, acc = carry
                s, values = scores_of(j)
                m2 = jnp.maximum(m, jnp.max(s, axis=1, keepdims=True))
                w = jnp.exp(s - m2)
                decay = jnp.exp(m - m2)
                l = l * decay + jnp.sum(w, axis=1, keepdims=True)
                acc = acc * decay + jnp.dot(
                    w.astype(jnp.bfloat16), values, preferred_element_type=jnp.float32
                )
                return m2, l, acc

            m, l, acc = lax.fori_loop(first, block, step, (m, l, acc))
            out = (acc / l).astype(jnp.bfloat16)
            for j in range(group_size):
                ctx_ref[rows, (kh * group_size + j) * HD:(kh * group_size + j + 1) * HD] = (
                    out[j * BLOCK:(j + 1) * BLOCK]
                )
        return 0

    lax.fori_loop(0, blk_dev, q_block, 0)


def on_device(
    hidden_states, norm_gain, w_query, w_key, w_value, prompt_blocks, owner_map, slot_table
):
    n_groups, n_dev, n_tp = (lax.axis_size(a) for a in ("groups", "dev", "tp"))
    device = lax.axis_index("dev")
    tok, feat = hidden_states.shape
    width = feat * n_tp
    q_width, kv_width = w_query.shape[1], w_key.shape[1]
    ny = n_dev // CORES
    blk_dev = owner_map.shape[0]

    token_rows = device * tok + jnp.arange(tok, dtype=jnp.int32)
    starts = jnp.sum(
        jnp.where(
            jnp.arange(prompt_blocks.shape[0])[None, :] < jnp.arange(prompt_blocks.shape[0])[:, None],
            prompt_blocks[None, :], 0), axis=1) * BLOCK
    start_of = jnp.max(
        jnp.where(token_rows[:, None] >= starts[None, :], starts[None, :], 0), axis=1)
    offsets = (token_rows - start_of).astype(jnp.float32)
    freq = jnp.arange(HD // 2, dtype=jnp.float32)
    inverse = jnp.exp(freq * (-2.0 * math.log(THETA) / HD))
    inverse = jnp.concatenate([inverse, inverse])
    sign = jnp.where(jnp.arange(HD) < HD // 2, -1.0, 1.0)
    angles = offsets[:, None] * inverse[None, :]
    cos2, sin2 = jnp.cos(angles), jnp.sin(angles) * sign[None, :]

    own = jnp.pad(owner_map[None, :], ((0, 7), (0, 128 - blk_dev)))
    q_chunks = 4 if ny == 2 else 1
    n_chunks = 2 + q_chunks
    pieces = 8 if n_tp == 4 else 2
    dma = pltpu.SemaphoreType.DMA
    far = max(ny - 1, 1)
    og = max(n_groups - 1, 1)
    hop = max(n_tp // 2, 1)
    vmem = pl.BlockSpec(memory_space=pltpu.VMEM)
    flops = 2 * tok * width * (q_width + 2 * kv_width)
    queries, kv_all, owners = pl.pallas_call(
        functools.partial(project_kernel, (n_groups, n_dev, n_tp, q_chunks, pieces)),
        out_shape=(
            jax.ShapeDtypeStruct((tok, q_width), jnp.bfloat16),
            jax.ShapeDtypeStruct((n_dev * tok, 2 * kv_width), jnp.bfloat16),
            jax.ShapeDtypeStruct((n_dev, 8, 128), jnp.int32),
        ),
        in_specs=[vmem] * 8,
        out_specs=(vmem, vmem, vmem),
        scratch_shapes=[
            pltpu.VMEM((tok, width), jnp.bfloat16),
            pltpu.VMEM((tok, width), jnp.bfloat16),
            pltpu.VMEM((width, q_width), jnp.bfloat16),
            pltpu.VMEM((width, kv_width), jnp.bfloat16),
            pltpu.VMEM((width, kv_width), jnp.bfloat16),
            pltpu.VMEM((n_dev * tok, 2 * kv_width), jnp.bfloat16),
            pltpu.VMEM((n_dev, 8, 128), jnp.int32),
            dma((5,)),
            dma((2, hop, pieces)), dma((2, hop, pieces)),
            dma((3,)), dma((3,)),
            dma((far, n_chunks)), dma((far, n_chunks)),
            dma((far, og, n_chunks)), dma((far, og, n_chunks)),
            dma((far, n_chunks)), dma((far, n_chunks)),
            dma((far, og, n_chunks)), dma((far, og, n_chunks)),
            dma((2, ny)), dma((2, ny)),
            dma((n_dev - 1,)), dma((n_dev - 1,)),
        ],
        cost_estimate=pl.CostEstimate(
            flops=flops, bytes_accessed=2 * width * (q_width + 2 * kv_width + tok),
            transcendentals=0),
        compiler_params=pltpu.CompilerParams(
            collective_id=0, has_side_effects=True, vmem_limit_bytes=VMEM_LIMIT),
    )(
        hidden_states, norm_gain.astype(jnp.float32)[None, :], w_query, w_key, w_value, cos2, sin2,
        own,
    )

    smem = pl.BlockSpec(memory_space=pltpu.SMEM)
    slots = slot_table.shape[1]
    return pl.pallas_call(
        functools.partial(attend_kernel, blk_dev, q_width // kv_width),
        out_shape=(
            jax.ShapeDtypeStruct((tok, q_width), jnp.bfloat16),
            jax.ShapeDtypeStruct((slots, BLOCK, 2 * kv_width), jnp.bfloat16),
        ),
        in_specs=[smem] * 4 + [vmem] * 2,
        out_specs=(vmem, vmem),
        compiler_params=pltpu.CompilerParams(vmem_limit_bytes=VMEM_LIMIT),
    )(
        prompt_blocks, owners[:, 0, :blk_dev].reshape(-1), slot_table[0],
        device.astype(jnp.int32)[None], queries, kv_all,
    )


def solution(mesh):
    in_specs = (
        P(("groups", "dev"), "tp"),
        P(),
        P("dev", "tp"),
        P("dev", "tp"),
        P("dev", "tp"),
        P("groups"),
        P(("groups", "dev")),
        P(("groups", "dev"), None),
    )
    out_specs = (P(("groups", "dev"), "tp"), P(("groups", "dev"), None, "tp"))
    return jax.shard_map(
        on_device, mesh=mesh, in_specs=in_specs, out_specs=out_specs, check_vma=False
    )
```

profile of v0, /device:TPU:22, one launch (start us, length us, event | category | flops | bytes accessed | tf_op | source)
XLA Modules:
  0.0 168.0 jit_solution(14983463414920979863)
XLA Ops:
  0.6 0.8 select_reduce_fusion.1
  1.4 0.1 compare_select_fusion
  1.5 1.3 pad.4.own_ref
  2.8 0.1 select_reduce_fusion
  2.9 1.3 broadcast_in_dim.59
  4.2 2.0 %fusion = (f32[640,128]{1,0:T(8,128)}, f32[640,128]{1,0:T(8,128)}) fusion(f32[128]{0:T(128)S(1)} %get-tuple-element.10, f32[128]{0:T(128)S(1)} %get-tuple-element.11, f32[640]{0:T(1024)S(1)} %subtract_convert_fusion), kind=kLoop, calls=%fused_computation.2 | loop fusion | flops 163840 | bytes 658944 | tf_op jit(solution)/shard_map/mul | solution.py:408
  6.2 146.5 %shard_map.95 = (bf16[640,1280]{1,0:T(8,128)(2,1)}, bf16[2560,512]{1,0:T(8,128)(2,1)}, s32[4,8,128]{2,1,0:T(8,128)}) custom-call(bf16[640,1280]{1,0:T(8,128)(2,1)} %h_ref.1, f32[1,5120]{1,0:T(1,128)} %bitcast.4, bf16[1280,1280]{1,0:T(8,128)(2,1)} %wq_ref.1, bf16[1280,256]{1,0:T(8,128)(2,1)} %wk_ref.1, bf16[1280,256]{1,0:T(8,128)(2,1)} %wv_ref.1, ...), custom_call_target="tpu_custom_call" | custom-call | flops 11744051200 | bytes 24903680 | tf_op jit(solution)/shard_map/pallas_call | solution.py:420
  152.7 0.7 slice_reduce_fusion
  153.4 0.6 reshape_squeeze.3.owner_ref
  154.0 14.0 %shard_map.96 = (bf16[640,1280]{1,0:T(8,128)(2,1)}, bf16[8,128,512]{2,1,0:T(8,128)(2,1)}) custom-call(s32[8]{0:T(128)} %prompt_ref.1, s32[20]{0:T(128)} %reshape_squeeze.3.owner_ref, s32[8]{0:T(128)} %bitcast.6, s32[1]{0:T(128)} %bitcast.3.dev_ref, bf16[640,1280]{1,0:T(8,128)(2,1)} %get-tuple-element.6.q_ref, bf16[2560,512]{1,0:T(8,128)(2,1)} %get-tuple-element.7.kv_ref), custom_call_target="tpu_custom_call" | custom-call | tf_op jit(solution)/shard_map/pallas_call | solution.py:459
  (4 shorter events, 0.0 us)
where the time goes:
time: 171 us; the launch traced here: 168 us
  Pallas kernels  160 us (94%)
  other arithmetic  4.31 us (3%)
  local copies, waits for them, and re-layouts  2.59 us (2%)
    pallas_call x1, Pallas kernels, on_device(): pl.pallas_call(functools.partial(project_kernel, (n_groups, n_dev, n_tp,...  146 us
    pallas_call x1, Pallas kernels, on_device(): pl.pallas_call(functools.partial(attend_kernel, blk_dev, q_width // kv_wi...  14 us

commit v1 on v0

--- a/solution.py
+++ b/solution.py
@@ -35,7 +35,10 @@
     kv_out,
     own_out,
     hid,
-    normed,
+    scaled,
+    squares,
+    q_acc,
+    kv_acc,
     wqf,
     wkf,
     wvf,
@@ -204,72 +207,124 @@
                 landed(part, xs_send.at[oy - 1, og - 1, k], xs_recv.at[oy - 1, og - 1, k],
                        {"dev": sib})
 
-    def h_step(s):
+    def h_relay(s, direction, p):
+        block = hid_piece(source(direction, s), p)
+        landed(block, h_send.at[direction, s - 1, p],
+               h_recv.at[direction, s - 1, p], {"tp": nbr[1 - direction]})
+        send(block, block, h_send.at[direction, s, p],
+             h_recv.at[direction, s, p], {"tp": nbr[direction]})
+
+    def h_last(s, direction, p):
+        landed(hid_piece(source(direction, s), p), h_send.at[direction, s - 1, p],
+               h_recv.at[direction, s - 1, p], {"tp": nbr[1 - direction]})
+
+    relays, lasts = [], []
+    reach = n_tp // 2
+    for s in range(1, reach + 1):
         for i in range(pieces):
             for direction in range(2):
                 p = order[direction][i]
                 if hops(direction, p) >= s + 1:
-                    block = hid_piece(source(direction, s), p)
-                    landed(block, h_send.at[direction, s - 1, p],
-                           h_recv.at[direction, s - 1, p], {"tp": nbr[1 - direction]})
-                    send(block, block, h_send.at[direction, s, p],
-                         h_recv.at[direction, s, p], {"tp": nbr[direction]})
-
+                    relays.append((s, direction, p))
+                elif hops(direction, p) == s:
+                    lasts.append((s, direction, p))
+
+    per = -(-len(relays) // q_chunks)
     y_step(*chunks[0])
     y_step(*chunks[1])
-    for s in range(1, n_tp // 2):
-        h_step(s)
     for i in range(2, len(chunks)):
         y_step(*chunks[i])
         x_step(*chunks[i - 2])
-    for i in range(pieces):
-        for direction in range(2):
-            p = order[direction][i]
-            s = hops(direction, p)
-            if s >= 1:
-                landed(hid_piece(source(direction, s), p), h_send.at[direction, s - 1, p],
-                       h_recv.at[direction, s - 1, p], {"tp": nbr[1 - direction]})
+        for relay in relays[(i - 2) * per:(i - 1) * per]:
+            h_relay(*relay)
+    for i in range(len(chunks) - 2, len(chunks)):
+        x_step(*chunks[i])
     for copy in locals_:
         copy.wait()
 
-    def norm_rows(i, _):
-        rows = pl.ds(pl.multiple_of(i * 16, 16), 16)
-        x = hid[rows, :].astype(jnp.float32)
-        square = jnp.sum(x * x, axis=1, keepdims=True) * (1.0 / (feat * n_tp))
-        normed[rows, :] = (x * lax.rsqrt(square + EPSILON) * gain_ref[...]).astype(jnp.bfloat16)
-        return 0
-
-    lax.fori_loop(0, tok // 16, norm_rows, 0)
+    step_rows = 16
+
+    def scale_rows(block, first, count, fresh):
+        columns = pl.ds(pl.multiple_of(block * feat, 128), feat)
+
+        def body(i, _):
+            rows = pl.ds(pl.multiple_of(first + i * step_rows, step_rows), step_rows)
+            x = hid[rows, columns].astype(jnp.float32)
+            total = jnp.broadcast_to(jnp.sum(x * x, axis=1, keepdims=True), (step_rows, HD))
+            squares[rows, :] = total if fresh else squares[rows, :] + total
+            scaled[rows, columns] = (x * gain_ref[:, columns]).astype(jnp.bfloat16)
+            return 0
+
+        lax.fori_loop(0, count // step_rows, body, 0)
+
+    def block_dot(block, w, columns):
+        k = pl.ds(pl.multiple_of(block * feat, 128), feat)
+        return jnp.dot(scaled[:, k], w[k, columns], preferred_element_type=jnp.float32)
+
+    scale_rows(t, 0, tok, True)
+    near = [t]
+    for s in range(1, reach):
+        for last in lasts:
+            if last[0] == s:
+                h_last(*last)
+        for direction in range(2):
+            block = source(direction, s)
+            near.append(block)
+            scale_rows(block, 0, tok, False)
 
     kv_width = wk_ref.shape[1]
     mine = pl.ds(pl.multiple_of(d * tok, tok), tok)
+    all_kv = pl.ds(0, kv_width)
+    for a in range(3):
+        landed(full_rows(a, sib), sib_send.at[a], sib_recv.at[a], {"dev": sib})
+    for chunk in chunks:
+        sib_done(*chunk)
+
+    q_width = wq_ref.shape[1]
+    tile = 256 if q_width % 256 == 0 else HD
+
+    def near_dot(w, columns):
+        total = block_dot(near[0], w, columns)
+        for block in near[1:]:
+            total = total + block_dot(block, w, columns)
+        return total
+
     for a in (0, 1):
-        landed(full_rows(a, sib), sib_send.at[a], sib_recv.at[a], {"dev": sib})
-        sib_done(*chunks[a])
-        proj = jnp.dot(normed[...], full_w[a][...], preferred_element_type=jnp.float32)
+        kv_acc[:, a * kv_width:(a + 1) * kv_width] = near_dot(full_w[a], all_kv)
+
+    def q_near(i, _):
+        columns = pl.ds(pl.multiple_of(i * tile, tile), tile)
+        q_acc[:, columns] = near_dot(wqf, columns)
+        return 0
+
+    lax.fori_loop(0, q_width // tile, q_near, 0)
+
+    far_block = source(0, reach)
+    for last in lasts:
+        if last[0] == reach:
+            h_last(*last)
+            scale_rows(far_block, last[2] * prow, prow, False)
+    squares[...] = lax.rsqrt(squares[...] * (1.0 / (feat * n_tp)) + EPSILON)
+
+    for a in (0, 1):
+        proj = kv_acc[:, a * kv_width:(a + 1) * kv_width] + block_dot(far_block, full_w[a], all_kv)
         for head in range(kv_width // HD):
-            part = proj[:, head * HD:(head + 1) * HD]
+            part = proj[:, head * HD:(head + 1) * HD] * squares[...]
             if a == 0:
                 part = rope(part, cos_ref[...], sin_ref[...])
             kvf[mine, (2 * head + a) * HD:(2 * head + a + 1) * HD] = part.astype(jnp.bfloat16)
-    for i in range(len(chunks) - 2, len(chunks)):
-        x_step(*chunks[i])
-    send(kvf.at[mine], kvf.at[mine], kv_send.at[0, 0], kv_recv.at[0, 0], {"dev": sib})
     for oy in range(1, ny):
         peer = ((y + oy) % ny) * CORES + core
         send(kvf.at[mine], kvf.at[mine], kv_send.at[0, oy], kv_recv.at[0, oy], {"dev": peer})
-    landed(full_rows(2, sib), sib_send.at[2], sib_recv.at[2], {"dev": sib})
-    for i in range(2, len(chunks)):
-        sib_done(*chunks[i])
-
-    q_width = wq_ref.shape[1]
-    tile = 256 if q_width % 256 == 0 else HD
+    send(kvf.at[mine], kvf.at[mine], kv_send.at[0, 0], kv_recv.at[0, 0], {"dev": sib})
 
     def q_tile(i, _):
         columns = pl.ds(pl.multiple_of(i * tile, tile), tile)
-        proj = jnp.dot(normed[...], wqf[:, columns], preferred_element_type=jnp.float32)
+        proj = q_acc[:, columns] + block_dot(far_block, wqf, columns)
         parts = [
-            rope(proj[:, j * HD:(j + 1) * HD], cos_ref[...], sin_ref[...]).astype(jnp.bfloat16)
+            rope(
+                proj[:, j * HD:(j + 1) * HD] * squares[...], cos_ref[...], sin_ref[...]
+            ).astype(jnp.bfloat16)
             for j in range(tile // HD)
         ]
         q_out[:, columns] = parts[0] if len(parts) == 1 else jnp.concatenate(parts, axis=1)
@@ -333,34 +388,41 @@
             first = jnp.where(total <= block, total, first)
             total = total + prompt_ref[p]
         rows = pl.ds(pl.multiple_of(b * BLOCK, BLOCK), BLOCK)
-        for kh in range(kv_heads):
-            q = jnp.concatenate(
+        q_heads = [
+            jnp.concatenate(
                 [
                     q_ref[rows, (kh * group_size + j) * HD:(kh * group_size + j + 1) * HD]
                     for j in range(group_size)
                 ],
                 axis=0,
             )
-
-            def scores_of(j):
-                at = pl.ds(pl.multiple_of(j * BLOCK, BLOCK), BLOCK)
-                keys = kv_ref[at, 2 * kh * HD:(2 * kh + 1) * HD]
-                values = kv_ref[at, (2 * kh + 1) * HD:(2 * kh + 2) * HD]
-                s = lax.dot_general(
-                    q, keys, (((1,), (1,)), ((), ())), preferred_element_type=jnp.float32
-                ) * scale
-                return s, values
-
-            s, values = scores_of(block)
+            for kh in range(kv_heads)
+        ]
+
+        def scores_of(j, kh):
+            at = pl.ds(pl.multiple_of(j * BLOCK, BLOCK), BLOCK)
+            keys = kv_ref[at, 2 * kh * HD:(2 * kh + 1) * HD]
+            values = kv_ref[at, (2 * kh + 1) * HD:(2 * kh + 2) * HD]
+            s = lax.dot_general(
+                q_heads[kh], keys, (((1,), (1,)), ((), ())), preferred_element_type=jnp.float32
+            ) * scale
+            return s, values
+
+        carry = []
+        for kh in range(kv_heads):
+            s, values = scores_of(block, kh)
             s = jnp.where(causal, s, -1e30)
             m = jnp.max(s, axis=1, keepdims=True)
-            w = jnp.where(causal, jnp.exp(s - m), 0.0)
+            w = jnp.exp(s - m)
             l = jnp.sum(w, axis=1, keepdims=True)
             acc = jnp.dot(w.astype(jnp.bfloat16), values, preferred_element_type=jnp.float32)
-
-            def step(j, carry):
-                m, l, acc = carry
-                s, values = scores_of(j)
+            carry.append((m, l, acc))
+
+        def step(j, carry):
+            new = []
+            for kh in range(kv_heads):
+                m, l, acc = carry[kh]
+                s, values = scores_of(j, kh)
                 m2 = jnp.maximum(m, jnp.max(s, axis=1, keepdims=True))
                 w = jnp.exp(s - m2)
                 decay = jnp.exp(m - m2)
@@ -368,9 +430,12 @@
                 acc = acc * decay + jnp.dot(
                     w.astype(jnp.bfloat16), values, preferred_element_type=jnp.float32
                 )
-                return m2, l, acc
-
-            m, l, acc = lax.fori_loop(first, block, step, (m, l, acc))
+                new.append((m2, l, acc))
+            return tuple(new)
+
+        carry = lax.fori_loop(first, block, step, tuple(carry))
+        for kh in range(kv_heads):
+            m, l, acc = carry[kh]
             out = (acc / l).astype(jnp.bfloat16)
             for j in range(group_size):
                 ctx_ref[rows, (kh * group_size + j) * HD:(kh * group_size + j + 1) * HD] = (
@@ -429,6 +494,9 @@
         scratch_shapes=[
             pltpu.VMEM((tok, width), jnp.bfloat16),
             pltpu.VMEM((tok, width), jnp.bfloat16),
+            pltpu.VMEM((tok, HD), jnp.float32),
+            pltpu.VMEM((tok, q_width), jnp.float32),
+            pltpu.VMEM((tok, 2 * kv_width), jnp.float32),
             pltpu.VMEM((width, q_width), jnp.bfloat16),
             pltpu.VMEM((width, kv_width), jnp.bfloat16),
             pltpu.VMEM((width, kv_width), jnp.bfloat16),

time: 171 us -> 158 us (0.924)
  Pallas kernels: 160 us -> 148 us
    pallas_call x1, Pallas kernels: 146 us -> 134 us  [on_device(): pl.pallas_call(functools.partial(project_kernel, (n_groups, n_dev, n_tp,...]
where the time goes in v1:
time: 158 us; the launch traced here: 155 us
  Pallas kernels  148 us (94%)
  other arithmetic  4.31 us (3%)
  local copies, waits for them, and re-layouts  2.59 us (2%)
    pallas_call x1, Pallas kernels, on_device(): pl.pallas_call(functools.partial(project_kernel, (n_groups, n_dev, n_tp,...  134 us
    pallas_call x1, Pallas kernels, on_device(): pl.pallas_call(functools.partial(attend_kernel, blk_dev, q_width // kv_wi...  13.3 us

profile of v1, /device:TPU:22, one launch (start us, length us, event | category | flops | bytes accessed | tf_op | source)
XLA Modules:
  0.0 155.1 jit_solution(8606041540252598851)
XLA Ops:
  0.6 0.8 select_reduce_fusion.1
  1.4 0.1 compare_select_fusion
  1.5 1.3 pad.4.own_ref
  2.8 0.1 select_reduce_fusion
  2.9 1.3 broadcast_in_dim.59
  4.2 2.0 %fusion = (f32[640,128]{1,0:T(8,128)}, f32[640,128]{1,0:T(8,128)}) fusion(f32[128]{0:T(128)S(1)} %get-tuple-element.10, f32[128]{0:T(128)S(1)} %get-tuple-element.11, f32[640]{0:T(1024)S(1)} %subtract_convert_fusion), kind=kLoop, calls=%fused_computation.2 | loop fusion | flops 163840 | bytes 658944 | tf_op jit(solution)/shard_map/mul | solution.py:473
  6.2 134.3 %shard_map.95 = (bf16[640,1280]{1,0:T(8,128)(2,1)}, bf16[2560,512]{1,0:T(8,128)(2,1)}, s32[4,8,128]{2,1,0:T(8,128)}) custom-call(bf16[640,1280]{1,0:T(8,128)(2,1)} %h_ref.1, f32[1,5120]{1,0:T(1,128)} %bitcast.4, bf16[1280,1280]{1,0:T(8,128)(2,1)} %wq_ref.1, bf16[1280,256]{1,0:T(8,128)(2,1)} %wk_ref.1, bf16[1280,256]{1,0:T(8,128)(2,1)} %wv_ref.1, ...), custom_call_target="tpu_custom_call" | custom-call | flops 11744051200 | bytes 24903680 | tf_op jit(solution)/shard_map/pallas_call | solution.py:485
  140.5 0.7 slice_reduce_fusion
  141.3 0.6 reshape_squeeze.3.owner_ref
  141.8 13.3 %shard_map.96 = (bf16[640,1280]{1,0:T(8,128)(2,1)}, bf16[8,128,512]{2,1,0:T(8,128)(2,1)}) custom-call(s32[8]{0:T(128)} %prompt_ref.1, s32[20]{0:T(128)} %reshape_squeeze.3.owner_ref, s32[8]{0:T(128)} %bitcast.6, s32[1]{0:T(128)} %bitcast.3.dev_ref, bf16[640,1280]{1,0:T(8,128)(2,1)} %get-tuple-element.6.q_ref, bf16[2560,512]{1,0:T(8,128)(2,1)} %get-tuple-element.7.kv_ref), custom_call_target="tpu_custom_call" | custom-call | tf_op jit(solution)/shard_map/pallas_call | solution.py:527
  (4 shorter events, 0.0 us)
